TPU v7x, 128 devices: a whole 4x4x4 slice. The times are simulated.
128 devices in a mesh: ctx: 16 (over x, z), head: 8 (over y, core).
Axes of the slice: x: 4, y: 4, z: 4, core: 2. Of those that a mesh axis runs over, the one named last changes fastest.
Arguments:
- input_x_channels: bfloat16 [16384, 8192], P('ctx', 'head'), may hold values from -4 to 4
- input_b_channels: bfloat16 [16384, 1024], P('ctx', 'head'), may hold values from -3 to 3
- input_c_channels: bfloat16 [16384, 1024], P('ctx', 'head'), may hold values from -3 to 3
- input_gate_channels: bfloat16 [16384, 8192], P('ctx', 'head'), may hold values from -75 to 75
- raw_step_sizes: float32 [128, 16384], P('head', 'ctx'), may hold values from -7 to 800
- log_decay_rate: float32 [128], P('head'), may hold values from -8 to -2.3
- head_skip_coeff: float32 [128], P('head'), may hold values from 0.5 to 2
- x_conv_taps: bfloat16 [4, 8192], P(None, 'head'), may hold values from -3 to 3
- b_conv_taps: bfloat16 [4, 1024], P(None, 'head'), may hold values from -3 to 3
- c_conv_taps: bfloat16 [4, 1024], P(None, 'head'), may hold values from -3 to 3
- gated_norm_gain: bfloat16 [8192], P('head'), may hold values from 0.099609375 to 1.8984375
- output_weight: bfloat16 [8192, 4096], P('head'), may hold values from -0.0625 to 0.0625
- adapter_down_panels: bfloat16 [96, 8192, 64], P('ctx', 'head'), may hold values from -0.0625 to 0.0625
- adapter_up_panels: bfloat16 [96, 64, 4096], P('ctx', None, 'head'), may hold values from -0.75 to 0.75
- turn_first_token: int32 [32], replicated, may hold values from 0 to 16256, as said below
- tenant_of_turn: int32 [32], replicated, may hold values from 0 to 95
- tenant_panel_index: int32 [96], replicated, may hold values from 0 to 95, each once
Outputs:
- out: bfloat16 [16384, 4096], P('ctx', 'head')
Inputs may be any that keep to these rules, and one draw needn't show every extreme that they name: `turn_first_token`: strictly increasing multiples of 128; the first is 0; every aligned block of 1024 tokens holds exactly 2 starts, and in every block but the first the earlier of them lies past the block's first token.
All inputs are finite; a program needn't handle non-finite values.
Results may differ from a plain program's by a relative error of at most 0.014.
Values may be sent and summed in bfloat16 or wider, within the bound.
A program may use at most 128 MiB of HBM per device.

v0:
```python
import jax
import jax.numpy as jnp
from jax import lax
from jax.sharding import PartitionSpec as P

P_SIZE = 64
N = 128
K = 4
Q = 128
TURN_DEV = 2
highest = lax.Precision.HIGHEST
epsilon = 1e-05


def shifted(block, axis, distance):
    devices = range(lax.axis_size(axis))
    route = [(i - distance, i) for i in devices if i - distance in devices]
    return lax.ppermute(block, axis, route)


def conv_rows(sequence, tail_rows, weight):
    token_rows = sequence.shape[0]
    joined = jnp.concatenate([tail_rows, sequence], axis=0).astype(jnp.float32)
    total = jnp.zeros((token_rows, sequence.shape[1]), jnp.float32)
    for tap in range(weight.shape[0]):
        total = total + weight[tap].astype(jnp.float32) * joined[tap : tap + token_rows]
    return jax.nn.silu(total).astype(jnp.bfloat16)


def local(
    input_x_channels,
    input_b_channels,
    input_c_channels,
    input_gate_channels,
    raw_step_sizes,
    log_decay_rate,
    head_skip_coeff,
    x_conv_taps,
    b_conv_taps,
    c_conv_taps,
    gated_norm_gain,
    output_weight,
    adapter_down_panels,
    adapter_up_panels,
    turn_first_token,
    tenant_of_turn,
    tenant_panel_index,
):
    token_rows = input_x_channels.shape[0]
    head_count = log_decay_rate.shape[0]
    group_count = input_b_channels.shape[1] // N
    per_group = head_count // group_count
    conv_edge = K - 1
    conv_tails = shifted(
        (
            input_x_channels[token_rows - conv_edge :],
            input_b_channels[token_rows - conv_edge :],
            input_c_channels[token_rows - conv_edge :],
        ),
        "ctx",
        1,
    )
    x_conv = conv_rows(input_x_channels, conv_tails[0], x_conv_taps)
    b_conv = conv_rows(input_b_channels, conv_tails[1], b_conv_taps)
    c_conv = conv_rows(input_c_channels, conv_tails[2], c_conv_taps)
    block_count = token_rows // Q
    step_sizes = jax.nn.softplus(raw_step_sizes)
    decay_rate = jnp.exp(log_decay_rate)
    step_heads = step_sizes.reshape(head_count, block_count, Q)
    running = jnp.cumsum(-step_heads * decay_rate[:, None, None], axis=2)
    run_blocks = running.transpose(1, 0, 2).reshape(block_count, group_count, per_group, Q)
    step_blocks = step_heads.transpose(1, 0, 2).reshape(block_count, group_count, per_group, Q)
    x_blocks = x_conv.astype(jnp.float32).reshape(block_count, Q, group_count, per_group, P_SIZE)
    b_blocks = b_conv.astype(jnp.float32).reshape(block_count, Q, group_count, N)
    c_blocks = c_conv.astype(jnp.float32).reshape(block_count, Q, group_count, N)
    scores = jnp.einsum("cqgn,ckgn->cgqk", c_blocks, b_blocks, precision=highest)
    causal = jnp.arange(Q)[:, None] >= jnp.arange(Q)[None, :]
    log_gap = run_blocks[..., :, None] - run_blocks[..., None, :]
    decay_mat = jnp.where(causal, jnp.exp(jnp.where(causal, log_gap, 0.0)), 0.0)
    mixing = scores[:, :, None] * decay_mat * step_blocks[..., None, :]
    y_local = jnp.einsum("cghqk,ckghp->cqghp", mixing, x_blocks, precision=highest)
    tail_weight = jnp.exp(run_blocks[..., -1:] - run_blocks) * step_blocks
    block_states = jnp.einsum(
        "cghk,ckghp,ckgn->cghpn", tail_weight, x_blocks, b_blocks, precision=highest
    )
    block_log = run_blocks[..., -1]

    def carry_step(carried, inputs):
        fresh_state, step_log = inputs
        return (jnp.exp(step_log)[..., None, None] * carried + fresh_state, carried)

    empty_state = jnp.zeros((group_count, per_group, P_SIZE, N), jnp.float32)
    device_state, before = lax.scan(carry_step, empty_state, (block_states, block_log))
    device_log = jnp.sum(block_log, axis=0)
    run_tokens = run_blocks.transpose(0, 3, 1, 2)
    y_local = y_local + jnp.exp(run_tokens)[..., None] * jnp.einsum(
        "cqgn,cghpn->cqghp", c_blocks, before, precision=highest
    )
    all_logs, states = (
        lax.all_gather(device_log[None], "ctx", axis=0, tiled=True),
        lax.all_gather(device_state[None], "ctx", axis=0, tiled=True),
    )
    device_count = all_logs.shape[0]
    own_index = lax.axis_index("ctx")
    order_index = jnp.arange(device_count)
    between = (order_index[:, None] < order_index[None, :]) & (order_index[None, :] < own_index)
    span_log = jnp.einsum("jk,kgh->jgh", between.astype(jnp.float32), all_logs, precision=highest)
    weights = jnp.where((order_index < own_index)[:, None, None], jnp.exp(span_log), 0.0)
    incoming = jnp.einsum("jgh,jghpn->ghpn", weights, states, precision=highest)
    start_log = jnp.cumsum(block_log, axis=0) - block_log
    device_running = start_log[:, None] + run_tokens
    y_value = y_local + jnp.exp(device_running)[..., None] * jnp.einsum(
        "cqgn,ghpn->cqghp", c_blocks, incoming, precision=highest
    )
    y_value = y_value + head_skip_coeff.reshape(group_count, per_group)[:, :, None] * x_blocks
    group_width = per_group * P_SIZE
    gated = y_value.reshape(token_rows, group_count, group_width) * jax.nn.silu(
        input_gate_channels.astype(jnp.float32)
    ).reshape(token_rows, group_count, group_width)
    norm_scale = lax.rsqrt(jnp.mean(gated * gated, axis=2, keepdims=True) + epsilon)
    y_normed = (
        (gated * norm_scale).reshape(token_rows, -1) * gated_norm_gain.astype(jnp.float32)
    ).astype(jnp.bfloat16)
    own_index = lax.axis_index("ctx")
    slot_count = TURN_DEV + 1
    slot_turns = TURN_DEV * own_index - 1 + jnp.arange(slot_count)
    clipped = jnp.maximum(slot_turns, 0)
    tenants = jnp.take(tenant_of_turn, clipped)
    slot_homes = jnp.take(tenant_panel_index, tenants)
    all_down, all_up = (
        lax.all_gather(adapter_down_panels, "ctx", axis=0, tiled=True),
        lax.all_gather(adapter_up_panels, "ctx", axis=0, tiled=True),
    )
    down_slots = jnp.take(all_down, slot_homes, axis=0)
    up_slots = jnp.take(all_up, slot_homes, axis=0)
    base_out = lax.psum_scatter(
        jnp.dot(y_normed, output_weight, preferred_element_type=jnp.float32).astype(jnp.bfloat16),
        "head",
        scatter_dimension=1,
        tiled=True,
    ).astype(jnp.float32)
    own_starts = lax.dynamic_slice_in_dim(turn_first_token, TURN_DEV * own_index, TURN_DEV, 0)
    token_place = own_index * token_rows + jnp.arange(token_rows)
    token_slot = jnp.sum((token_place[:, None] >= own_starts[None, :]).astype(jnp.int32), axis=1)
    slot_mask = (token_slot[:, None] == jnp.arange(slot_count)[None, :]).astype(jnp.float32)
    low_slots = jnp.einsum("tc,scr->tsr", y_normed, down_slots, preferred_element_type=jnp.float32)
    rank_reduced = jnp.sum(low_slots * slot_mask[:, :, None], axis=1)
    rank_reduced = lax.psum(rank_reduced, "head").astype(jnp.bfloat16)
    adapter_out = jnp.einsum(
        "tr,srd->tsd", rank_reduced, up_slots, preferred_element_type=jnp.float32
    )
    adapter_out = jnp.sum(adapter_out * slot_mask[:, :, None], axis=1)
    return (base_out + adapter_out).astype(jnp.bfloat16)


def solution(mesh):
    in_specs = (
        P("ctx", "head"),
        P("ctx", "head"),
        P("ctx", "head"),
        P("ctx", "head"),
        P("head", "ctx"),
        P("head"),
        P("head"),
        P(None, "head"),
        P(None, "head"),
        P(None, "head"),
        P("head"),
        P("head", None),
        P("ctx", "head", None),
        P("ctx", None, "head"),
        P(),
        P(),
        P(),
    )
    out_specs = P("ctx", "head")
    return jax.shard_map(local, mesh=mesh, in_specs=in_specs, out_specs=out_specs, check_vma=False)
```

profile of v0, /device:TPU:0, one launch (start us, length us, event | category | flops | bytes accessed | tf_op | source)
XLA Modules:
  0.0 349.8 jit_solution(5705735439827553091)
XLA Ops:
  6.5 0.8 slice.86
  7.3 0.9 copy.74
  8.2 3.9 %collective-permute-start = (bf16[3,1024]{0,1:T(8,128)(2,1)}, bf16[3,1024]{0,1:T(8,128)(2,1)S(1)}, u32[]{:S(2)}, u32[]{:S(2)}) collective-permute-start(bf16[3,1024]{0,1:T(8,128)(2,1)} %copy.74), channel_id=1, source_target_pairs={{0,8},{8,16},{16,24},{24,32},{32,40},{40,48},{48,56},{56,64},{64,7... | collective-permute-start | bytes 18440 | tf_op jit(solution)/shard_map/ppermute | solution.py:18
  12.1 0.7 slice.104
  12.8 3.8 %collective-permute-start.2 = (bf16[3,128]{1,0:T(4,128)(2,1)S(1)}, bf16[3,128]{1,0:T(4,128)(2,1)S(1)}, u32[]{:S(2)}, u32[]{:S(2)}) collective-permute-start(bf16[3,128]{1,0:T(4,128)(2,1)S(1)} %slice.104), channel_id=1, source_target_pairs={{0,8},{8,16},{16,24},{24,32},{32,40},{40,48},{48,56},{56,64},{64,7... | collective-permute-start | bytes 2312 | tf_op jit(solution)/shard_map/ppermute | solution.py:18
  16.6 0.9 slice_convert_fusion.3
  17.5 0.9 fusion.48
  18.4 0.7 exp.63
  19.1 4.5 %reduce_window_sum.22 = f32[16,8,128]{2,1,0:T(8,128)S(1)} reduce-window(f32[16,8,128]{2,1,0:T(8,128)S(1)} %negate_multiply_fusion, f32[]{:T(128)} %constant.95.clone.1), window={size=1x1x128 pad=0_0x0_0x127_0}, to_apply=%region_0.1 | reduce-window | flops 2080768 | bytes 131076 | tf_op jit(solution)/shard_map/jit(cumsum)/reduce_window_sum | solution.py:70
  24.2 0.8 bitcast_convert_fusion.3
  25.0 2.9 copy.75
  28.1 0.3 multiply_convert_fusion.2
  28.5 1.2 maximum_convert_fusion
  29.7 5.5 %convert_bitcast_fusion = (f32[128,8,8,128]{3,1,2,0:T(8,128)}, bf16[1024,1024]{0,1:T(8,128)(2,1)S(1)}) fusion(f32[1027,1024]{0,1:T(8,128)S(1)} %maximum_convert_fusion, f32[1024]{0:T(1024)S(1)} %bitcast.186, f32[1024]{0:T(1024)S(1)} %bitcast.187, f32[1024]{0:T(1024)S(1)} %bitcast.185, f32[1024]{0:T(1024)S(1)} %bitcast.184), kind=kLoop, calls=%fused_computation.43 | loop fusion | flops 13631488 | bytes 23085056
  35.2 0.6 copy.102
  35.8 0.4 convert_multiply_fusion.1
  36.2 3.8 %fusion.31 = f32[8,1,16,64,128]{4,3,2,1,0:T(8,128)} fusion(bf16[8,128,128,1]{2,1,3,0:T(8,128)(2,1)S(1)} %bitcast.173, f32[8,128,16,64]{1,0,3,2:T(8,128)S(1)} %convert_multiply_fusion.1), kind=kOutput, calls=%fused_computation.55 | convolution fusion | flops 1610612736 | bytes 8650752 | tf_op jit(solution)/shard_map/cghk,ckghp,ckgn->cghpn/dot_general | solution.py:83
  40.0 16.3 %while.13 = (s32[]{:T(128)}, f32[1,16,64,128]{3,2,1,0:T(8,128)S(1)}, f32[8,1,16,64,128]{4,3,2,1,0:T(8,128)}, f32[8,1,16]{2,1,0:T(1,128)S(1)}, f32[8,1,16,64,128]{4,3,2,1,0:T(8,128)}, /*index=5*/s32[]{:T(128)}, s32[]{:T(128)}) while((s32[]{:T(128)}, f32[1,16,64,128]{3,2,1,0:T(8,128)S(1)}, f32[8,1,16,64,128]{4,3,2,1,0:T(8,128)}, ...), condition=%wide.region_2.3_spmd.clone, body=%wide.region_1.2_spmd.clone.sunk | while | flops 524291 | bytes 2622240 | solution.py:93
  40.0 0.8 bitcast_dynamic-update-slice_fusion.2
  40.9 1.2 bitcast_add_fusion.2
  42.0 0.9 bitcast_dynamic-update-slice_fusion.2
  42.9 1.2 bitcast_add_fusion.2
  44.1 0.9 bitcast_dynamic-update-slice_fusion.2
  45.0 1.2 bitcast_add_fusion.2
  46.1 0.8 bitcast_dynamic-update-slice_fusion.2
  47.0 1.2 bitcast_add_fusion.2
  48.2 0.8 bitcast_dynamic-update-slice_fusion.2
  49.0 1.2 bitcast_add_fusion.2
  50.2 0.9 bitcast_dynamic-update-slice_fusion.2
  51.1 1.2 bitcast_add_fusion.2
  52.3 0.9 bitcast_dynamic-update-slice_fusion.2
  53.1 1.2 bitcast_add_fusion.2
  54.3 0.8 bitcast_dynamic-update-slice_fusion.2
  55.1 1.2 bitcast_add_fusion.2
  56.3 0.8 copy-done.2
  57.2 0.7 all-gather.8.cloned.1.call-update
  57.9 0.7 all-gather.6.cloned.1.call-update
  58.7 3.5 %collective-permute-start.1 = (bf16[3,128]{1,0:T(4,128)(2,1)S(1)}, bf16[3,128]{1,0:T(4,128)(2,1)S(1)}, u32[]{:S(2)}, u32[]{:S(2)}) collective-permute-start(bf16[3,128]{1,0:T(4,128)(2,1)S(1)} %slice.95), channel_id=1, source_target_pairs={{0,8},{8,16},{16,24},{24,32},{32,40},{40,48},{48,56},{56,64},{64,7... | collective-permute-start | bytes 2312 | tf_op jit(solution)/shard_map/ppermute | solution.py:18
  62.3 0.7 dynamic-slice
  63.9 36.2 %all-reduce = f32[256]{0:T(256)S(1)} all-reduce(f32[256]{0:T(256)S(1)} %dynamic-update-slice), channel_id=2, replica_groups=mesh['ctx'=16,'head'=8] {'ctx'}, use_global_device_ids=true, to_apply=%add | all-reduce | flops 256 | bytes 2048
  100.7 4.0 %copy.92 = bf16[1024,1024]{0,1:T(8,128)(2,1)} copy(bf16[1024,1024]{1,0:T(8,128)(2,1)} %param.22) | data formatting | bytes 4194304 | tf_op args[3]
  104.7 0.3 multiply_convert_fusion.3
  105.4 1.5 copy-done.3
  106.9 3.0 copy.104
  110.1 3.5 %fusion.21 = f32[8,16,64,128]{3,2,1,0:T(8,128)} fusion(bf16[8,128,128,1]{2,1,3,0:T(8,128)(2,1)S(1)} %bitcast.170, f32[8,1,16,64,128]{4,3,2,1,0:T(8,128)S(1)} %copy-done.8), kind=kOutput, calls=%fused_computation.38 | convolution fusion | flops 1610612736 | bytes 8650752 | tf_op jit(solution)/shard_map/cqgn,cghpn->cqghp/dot_general | solution.py:96
  113.6 11.3 %fusion.4 = f32[8,16,64,128]{3,2,1,0:T(8,128)} fusion(f32[8,16,128]{2,1,0:T(8,128)S(1)} %copy.78, f32[8,16,128]{2,1,0:T(8,128)S(1)} %copy.76, f32[8,128,128]{2,1,0:T(8,128)S(1)} %fusion.61, pred[128,128]{1,0:T(8,128)(4,1)S(1)} %iota_compare_fusion, bf16[8,128,16,64]{1,0,3,2:T(8,128)(2,1)S(1)} %bitcast.167), kind=kOutput, calls=%fused_computation.11 | convolution fusion | flops 1621098496 | bytes 6963200 | tf_op jit(solution)/shard_map/cghqk,ckghp->cqghp/dot_general | solution.py:81
  124.9 3.8 %all-gather.10.cloned.1.call-done = f32[16,16,64,128]{3,2,1,0:T(8,128)} async-done(((f32[1,16,64,128]{3,2,1,0:T(8,128)}), f32[16,16,64,128]{3,2,1,0:T(8,128)}) %all-gather.10.cloned.1.call-update) | async-done | bytes 8388624 | tf_op jit(solution)/shard_map/all_gather | solution.py:101
  128.7 12.8 %fusion.2 = f32[16,1,64,128]{3,1,2,0:T(1,128)S(1)} fusion(f32[16,16,1,1]{0,2,3,1:T(1,128)S(1)} %copy.96, f32[16,16,64,128]{3,2,1,0:T(8,128)} %all-gather.10.cloned.1.call-done), kind=kOutput, calls=%fused_computation.9 | convolution fusion | flops 25165824 | bytes 8913920 | tf_op jit(solution)/shard_map/jgh,jghpn->ghpn/dot_general | solution.py:109
  141.5 5.1 %fusion.19 = f32[8,128,1,16,64]{1,4,3,0,2:T(8,128)S(1)} fusion(f32[8,16,64,128]{3,2,1,0:T(8,128)S(1)} %copy-done.6, f32[8,16,64,128]{3,2,1,0:T(8,128)} %fusion.4, f32[8,128,1,16,64]{1,0,4,3,2:T(8,128)S(1)} %bitcast.164, f32[16,64,128,1]{2,1,0,3:T(8,128)S(1)} %bitcast.175, bf16[8,128,128,1]{2,1,3,0:T(8,128)(2,1)S(1)} %bitcast.171, f32[16]{0:T(128)S(1)} %copy-done.13, ...), kind=kOutput, calls=%fused_computation.35 | convolution fusion | flops 1616904192 | bytes 17694784 | tf_op jit(solution)/shard_map/cqgn,ghpn->cqghp/dot_general | solution.py:112
  146.6 3.3 copy.91
  150.0 1.7 multiply_reduce_fusion.1
  151.8 2.0 copy-done.4
  153.8 11.5 %convolution_convert_fusion = bf16[1024,4096]{1,0:T(8,128)(2,1)} fusion(bf16[1024,4096]{1,0:T(8,128)(2,1)S(1)} %bitcast.189, f32[1024,1024]{0,1:T(8,128)S(1)} %get-tuple-element.84, f32[1024]{0:T(1024)S(1)} %convert_element_type.84, f32[1024]{0:T(1024)S(1)} %add_rsqrt_fusion), kind=kOutput, calls=%fused_computation.18 | convolution fusion | flops 8597274624 | bytes 20979712 | tf_op jit(solution)/shard_map/dot_general | solution.py:137
  165.4 0.6 gather_fusion
  166.0 0.6 gather_fusion.1
  166.9 24.9 %all-gather.8.cloned.1.call-done = bf16[96,64,512]{2,1,0:T(8,128)(2,1)} async-done(((bf16[6,64,512]{2,1,0:T(8,128)(2,1)}), bf16[96,64,512]{2,1,0:T(8,128)(2,1)}) %all-gather.8.cloned.1.call-update) | async-done | bytes 6291472 | tf_op jit(solution)/shard_map/all_gather | solution.py:132
  191.8 3.3 gather_fusion.3
  195.1 88.6 %all-gather.6.cloned.1.call-done = bf16[96,1024,64]{1,2,0:T(8,128)(2,1)} async-done(((bf16[6,1024,64]{1,2,0:T(8,128)(2,1)}), bf16[96,1024,64]{1,2,0:T(8,128)(2,1)}) %all-gather.6.cloned.1.call-update) | async-done | bytes 12582928 | tf_op jit(solution)/shard_map/all_gather | solution.py:131
  283.7 5.1 %gather_fusion.2 = bf16[3,1024,64]{1,2,0:T(8,128)(2,1)S(1)} fusion(bf16[96,1024,64]{1,2,0:T(8,128)(2,1)} %all-gather.6.cloned.1.call-done, s32[1024]{0:T(1024)S(1)} %pad_clamp_fusion), kind=kCustom, calls=%fused_computation.2 | custom fusion | bytes 786444 | tf_op jit(solution)/shard_map/jit(_take)/gather | solution.py:134
  289.0 2.9 fusion.59
  291.9 31.3 %all-reduce.2 = bf16[1024,64]{0,1:T(8,128)(2,1)S(1)} all-reduce(f32[1024,64]{0,1:T(8,128)S(1)} %multiply_reduce_fusion.2), channel_id=1, replica_groups=mesh['ctx'=16,'head'=8] {'head'}, use_global_device_ids=true, to_apply=%region_9.10 | all-reduce | flops 65536 | bytes 393216 | tf_op jit(solution)/shard_map/psum | solution.py:148
  323.2 1.0 multiply_reduce_fusion
  324.3 16.4 %reduce-scatter.2.cloned.1.call-done = bf16[1024,512]{1,0:T(8,128)(2,1)} async-done(((bf16[1024,4096]{1,0:T(8,128)(2,1)}), bf16[1024,512]{1,0:T(8,128)(2,1)}) %reduce-scatter.2.cloned.1.call-update) | async-done | bytes 1048592 | tf_op jit(solution)/shard_map/reduce_scatter | solution.py:136
  340.7 2.6 add_convert_fusion
  (94 shorter events, 2.8 us)
Async XLA Ops:
  6.5 158.8 %copy-start = (s32[32]{0:T(128)S(1)}, s32[32]{0:T(128)}, u32[]{:S(2)}) copy-start(s32[32]{0:T(128)} %param.34) | copy-start | bytes 388
  6.5 21.5 %copy-start.9 = (bf16[1024,128]{1,0:T(8,128)(2,1)S(1)}, bf16[1024,128]{1,0:T(8,128)(2,1)}, u32[]{:S(2)}) copy-start(bf16[1024,128]{1,0:T(8,128)(2,1)} %param.20) | copy-start | bytes 786436
  6.5 122.1 %all-gather.10.cloned.1.call-start = ((), (), s32[]{:S(2)}) async-start(), calls=%async_computation.4 | async-start | bytes 8912896 | tf_op jit(solution)/shard_map/all_gather | solution.py:101
  8.2 20.3 %collective-permute-start = (bf16[3,1024]{0,1:T(8,128)(2,1)}, bf16[3,1024]{0,1:T(8,128)(2,1)S(1)}, u32[]{:S(2)}, u32[]{:S(2)}) collective-permute-start(bf16[3,1024]{0,1:T(8,128)(2,1)} %copy.74), channel_id=1, source_target_pairs={{0,8},{8,16},{16,24},{24,32},{32,40},{40,48},{48,56},{56,64},{64,7... | collective-permute-start | bytes 18440 | tf_op jit(solution)/shard_map/ppermute | solution.py:18
  12.8 15.2 %collective-permute-start.2 = (bf16[3,128]{1,0:T(4,128)(2,1)S(1)}, bf16[3,128]{1,0:T(4,128)(2,1)S(1)}, u32[]{:S(2)}, u32[]{:S(2)}) collective-permute-start(bf16[3,128]{1,0:T(4,128)(2,1)S(1)} %slice.104), channel_id=1, source_target_pairs={{0,8},{8,16},{16,24},{24,32},{32,40},{40,48},{48,56},{56,64},{64,7... | collective-permute-start | bytes 2312 | tf_op jit(solution)/shard_map/ppermute | solution.py:18
  40.0 18.7 %copy-start.10 = (bf16[1024,128]{1,0:T(8,128)(2,1)S(1)}, bf16[1024,128]{1,0:T(8,128)(2,1)}, u32[]{:S(2)}) copy-start(bf16[1024,128]{1,0:T(8,128)(2,1)} %param.21) | copy-start | bytes 786436
  40.0 22.2 %copy-start.15 = (u32[128]{0:T(128)S(1)}, u32[128]{0:T(128)}, u32[]{:S(2)}) copy-start(u32[128]{0:T(128)} %constant.114) | copy-start | bytes 1540
  40.0 60.3 %copy-start.11 = (bf16[4,128]{1,0:T(4,128)(2,1)S(1)}, bf16[4,128]{1,0:T(4,128)(2,1)}, u32[]{:S(2)}) copy-start(bf16[4,128]{1,0:T(4,128)(2,1)} %param.28) | copy-start | bytes 3076
  56.3 0.8 copy-start.2
  56.3 48.3 %copy-start.12 = (bf16[1024]{0:T(1024)(128)(2,1)S(1)}, bf16[1024]{0:T(1024)(128)(2,1)}, u32[]{:S(2)}) copy-start(bf16[1024]{0:T(1024)(128)(2,1)} %param.29) | copy-start | bytes 6148
  57.1 134.6 %all-gather.8.cloned.1.call-start = ((), (), s32[]{:S(2)}) async-start(), calls=%async_computation.3 | async-start | bytes 6684672 | tf_op jit(solution)/shard_map/all_gather | solution.py:132
  57.9 225.8 %all-gather.6.cloned.1.call-start = ((), (), s32[]{:S(2)}) async-start(), calls=%async_computation.2 | async-start | bytes 13369344 | tf_op jit(solution)/shard_map/all_gather | solution.py:131
  58.6 282.1 %reduce-scatter.2.cloned.1.call-start = ((), (), s32[]{:S(2)}) async-start(), calls=%async_computation.1 | async-start | bytes 9437184 | tf_op jit(solution)/shard_map/reduce_scatter | solution.py:136
  58.7 46.0 %collective-permute-start.1 = (bf16[3,128]{1,0:T(4,128)(2,1)S(1)}, bf16[3,128]{1,0:T(4,128)(2,1)S(1)}, u32[]{:S(2)}, u32[]{:S(2)}) collective-permute-start(bf16[3,128]{1,0:T(4,128)(2,1)S(1)} %slice.95), channel_id=1, source_target_pairs={{0,8},{8,16},{16,24},{24,32},{32,40},{40,48},{48,56},{56,64},{64,7... | collective-permute-start | bytes 2312 | tf_op jit(solution)/shard_map/ppermute | solution.py:18
  104.6 2.2 copy-start.3
  106.9 3.2 copy-start.8
  124.9 16.7 %copy-start.13 = (f32[16]{0:T(128)S(1)}, f32[16]{0:T(128)}, u32[]{:S(2)}) copy-start(f32[16]{0:T(128)} %param.25) | copy-start | bytes 196
  128.7 12.9 %copy-start.5 = (f32[128,8,8,128]{3,2,1,0:T(8,128)S(1)}, f32[128,8,8,128]{3,2,1,0:T(8,128)}, u32[]{:S(2)}) copy-start(f32[128,8,8,128]{3,2,1,0:T(8,128)} %copy.104) | copy-start | bytes 12582916
  128.7 12.9 %copy-start.6 = (f32[8,16,64,128]{3,2,1,0:T(8,128)S(1)}, f32[8,16,64,128]{3,2,1,0:T(8,128)}, u32[]{:S(2)}) copy-start(f32[8,16,64,128]{3,2,1,0:T(8,128)} %fusion.21) | copy-start | bytes 12582916
  146.6 3.3 copy-start.7
  146.6 7.2 %slice-start = ((s8[8388608]{0:T(1024)(128)(4,1)}), s8[4194304]{0:T(1024)(128)(4,1)S(1)}, s32[]{:S(2)}) async-start(s8[8388608]{0:T(1024)(128)(4,1)} %bitcast.188), calls=%async_computation.5 | async-start | bytes 8388608
  150.0 3.8 %slice-start.1 = ((s8[8388608]{0:T(1024)(128)(4,1)}), s8[4194304]{0:T(1024)(128)(4,1)S(1)}, s32[]{:S(2)}) async-start(s8[8388608]{0:T(1024)(128)(4,1)} %bitcast.188), calls=%async_computation.6 | async-start | bytes 8388608
  151.7 2.0 copy-start.4
  165.3 0.7 copy-start.1
  165.3 1.4 copy-start.14
Sparse Core Ops, SparseCore 0:
  57.3 71.3 all-gather.9
  130.8 60.8 all-gather.7
  194.0 89.7 all-gather.5
  286.0 54.6 reduce-scatter.1
where the time goes:
time: 351 us; the launch traced here: 350 us
  waiting for transfers between devices  135 us (38%)
  blocking collectives  67.5 us (19%)
  matrix products  52.3 us (15%)
  other arithmetic  36.4 us (10%)
  local copies, waits for them, and re-layouts  32.7 us (9%)
  between operations  14.3 us (4%)
  starting transfers between devices  11.4 us (3%)
    all_gather x1, waiting for transfers between devices, local(): lax.all_gather(adapter_down_panels, 'ctx', axis=0, tiled=True)  88.6 us
    unnamed x1, blocking collectives  36.2 us
    psum x1, blocking collectives, local(): rank_reduced = lax.psum(rank_reduced, 'head').astype(jnp.bfloat16)  31.3 us
    all_gather x1, waiting for transfers between devices, local(): lax.all_gather(adapter_up_panels, 'ctx', axis=0, tiled=True)  24.9 us
    reduce_scatter x1, waiting for transfers between devices, local(): lax.psum_scatter(jnp.dot(y_normed, output_weight, preferred_element_type=...  16.4 us
    unnamed x44, local copies, waits for them, and re-layouts  15.9 us
    dot_general x1, matrix products, local(): incoming = jnp.einsum('jgh,jghpn->ghpn', weights, states, precision=highest)  12.8 us
    dot_general x1, matrix products, local(): jnp.dot(y_normed, output_weight, preferred_element_type=jnp.float32)  11.5 us
  transfers between devices with their start and end apart: 7, of which 4 were waited for; matrix products, arithmetic and copies ran while one was open for 24% of the time, Pallas kernels for 0%

commit v1 on v0

--- a/solution.py
+++ b/solution.py
@@ -145,7 +145,7 @@
     slot_mask = (token_slot[:, None] == jnp.arange(slot_count)[None, :]).astype(jnp.float32)
     low_slots = jnp.einsum("tc,scr->tsr", y_normed, down_slots, preferred_element_type=jnp.float32)
     rank_reduced = jnp.sum(low_slots * slot_mask[:, :, None], axis=1)
-    rank_reduced = lax.psum(rank_reduced, "head").astype(jnp.bfloat16)
+    rank_reduced = jnp.sum(lax.all_gather(rank_reduced, "head"), axis=0).astype(jnp.bfloat16)
     adapter_out = jnp.einsum(
         "tr,srd->tsd", rank_reduced, up_slots, preferred_element_type=jnp.float32
     )

time: 351 us -> 376 us (1.071)
  waiting for transfers between devices: 135 us -> 182 us
  blocking collectives: 67.5 us -> 36.2 us
  matrix products: 52.3 us -> 56.6 us
    reduce_scatter x1, waiting for transfers between devices: 16.4 us -> 50.5 us  [local(): lax.psum_scatter(jnp.dot(y_normed, output_weight, preferred_element_type=...]
    psum x1 -> x0, blocking collectives: 31.3 us -> none  [local(): rank_reduced = lax.psum(rank_reduced, 'head').astype(jnp.bfloat16)]
    all_gather x0 -> x1, waiting for transfers between devices: none -> 23 us  [local(): lax.all_gather(rank_reduced, 'head')]
    all_gather x1, waiting for transfers between devices: 88.6 us -> 66.4 us  [local(): lax.all_gather(adapter_down_panels, 'ctx', axis=0, tiled=True)]
    all_gather x1, waiting for transfers between devices: 24.9 us -> 38.6 us  [local(): lax.all_gather(adapter_up_panels, 'ctx', axis=0, tiled=True)]
    dot_general x1, matrix products: 11.5 us -> 15.6 us  [local(): jnp.dot(y_normed, output_weight, preferred_element_type=jnp.float32)]
    unnamed x44 -> x41, local copies, waits for them, and re-layouts: 15.9 us -> 16.7 us
  transfers between devices with their start and end apart: 7 -> 8, of which waited for: 4 -> 5; matrix products, arithmetic and copies ran while one was open for 24% -> 26% of each run, Pallas kernels for 0% -> 0%
where the time goes in v1:
time: 376 us; the launch traced here: 374 us
  waiting for transfers between devices  182 us (48%)
  matrix products  56.6 us (15%)
  other arithmetic  40.1 us (11%)
  blocking collectives  36.2 us (10%)
  local copies, waits for them, and re-layouts  33.5 us (9%)
  between operations  14.2 us (4%)
  starting transfers between devices  11.4 us (3%)
    all_gather x1, waiting for transfers between devices, local(): lax.all_gather(adapter_down_panels, 'ctx', axis=0, tiled=True)  66.4 us
    reduce_scatter x1, waiting for transfers between devices, local(): lax.psum_scatter(jnp.dot(y_normed, output_weight, preferred_element_type=...  50.5 us
    all_gather x1, waiting for transfers between devices, local(): lax.all_gather(adapter_up_panels, 'ctx', axis=0, tiled=True)  38.6 us
    unnamed x1, blocking collectives  36.2 us
    all_gather x1, waiting for transfers between devices, local(): lax.all_gather(rank_reduced, 'head')  23 us
    unnamed x41, local copies, waits for them, and re-layouts  16.7 us
    dot_general x1, matrix products, local(): jnp.dot(y_normed, output_weight, preferred_element_type=jnp.float32)  15.6 us
    dot_general x1, matrix products, local(): incoming = jnp.einsum('jgh,jghpn->ghpn', weights, states, precision=highest)  12.8 us
  transfers between devices with their start and end apart: 8, of which 5 were waited for; matrix products, arithmetic and copies ran while one was open for 26% of the time, Pallas kernels for 0%

profile of v1, /device:TPU:0, one launch (start us, length us, event | category | flops | bytes accessed | tf_op | source)
XLA Modules:
  0.0 374.3 jit_solution(16101727310976549852)
XLA Ops:
  6.5 0.8 slice.86
  7.3 0.9 copy.73
  8.2 3.9 %collective-permute-start = (bf16[3,1024]{0,1:T(8,128)(2,1)}, bf16[3,1024]{0,1:T(8,128)(2,1)S(1)}, u32[]{:S(2)}, u32[]{:S(2)}) collective-permute-start(bf16[3,1024]{0,1:T(8,128)(2,1)} %copy.73), channel_id=1, source_target_pairs={{0,8},{8,16},{16,24},{24,32},{32,40},{40,48},{48,56},{56,64},{64,7... | collective-permute-start | bytes 18440 | tf_op jit(solution)/shard_map/ppermute | solution.py:18
  12.1 0.7 slice.104
  12.8 3.8 %collective-permute-start.2 = (bf16[3,128]{1,0:T(4,128)(2,1)S(1)}, bf16[3,128]{1,0:T(4,128)(2,1)S(1)}, u32[]{:S(2)}, u32[]{:S(2)}) collective-permute-start(bf16[3,128]{1,0:T(4,128)(2,1)S(1)} %slice.104), channel_id=1, source_target_pairs={{0,8},{8,16},{16,24},{24,32},{32,40},{40,48},{48,56},{56,64},{64,7... | collective-permute-start | bytes 2312 | tf_op jit(solution)/shard_map/ppermute | solution.py:18
  16.6 0.9 slice_convert_fusion.3
  17.5 0.9 fusion.48
  18.4 0.7 exp.63
  19.1 4.5 %reduce_window_sum.22 = f32[16,8,128]{2,1,0:T(8,128)S(1)} reduce-window(f32[16,8,128]{2,1,0:T(8,128)S(1)} %negate_multiply_fusion, f32[]{:T(128)} %constant.95.clone.1), window={size=1x1x128 pad=0_0x0_0x127_0}, to_apply=%region_0.1 | reduce-window | flops 2080768 | bytes 131076 | tf_op jit(solution)/shard_map/jit(cumsum)/reduce_window_sum | solution.py:70
  24.2 0.8 bitcast_convert_fusion.3
  25.0 2.9 copy.74
  28.5 1.2 maximum_convert_fusion
  29.7 5.4 %convert_bitcast_fusion = (f32[128,8,8,128]{3,1,2,0:T(8,128)}, bf16[1024,1024]{0,1:T(8,128)(2,1)S(1)}) fusion(f32[1027,1024]{0,1:T(8,128)S(1)} %maximum_convert_fusion, f32[1024]{0:T(1024)S(1)} %bitcast.192, f32[1024]{0:T(1024)S(1)} %bitcast.193, f32[1024]{0:T(1024)S(1)} %bitcast.191, f32[1024]{0:T(1024)S(1)} %bitcast.190), kind=kLoop, calls=%fused_computation.43 | loop fusion | flops 13631488 | bytes 23085056
  35.1 0.6 copy.101
  35.8 0.4 convert_multiply_fusion.1
  36.2 3.8 %fusion.31 = f32[8,1,16,64,128]{4,3,2,1,0:T(8,128)} fusion(bf16[8,128,128,1]{2,1,3,0:T(8,128)(2,1)S(1)} %bitcast.178, f32[8,128,16,64]{1,0,3,2:T(8,128)S(1)} %convert_multiply_fusion.1), kind=kOutput, calls=%fused_computation.55 | convolution fusion | flops 1610612736 | bytes 8650752 | tf_op jit(solution)/shard_map/cghk,ckghp,ckgn->cghpn/dot_general | solution.py:83
  40.0 16.3 %while.13 = (s32[]{:T(128)}, f32[1,16,64,128]{3,2,1,0:T(8,128)S(1)}, f32[8,1,16,64,128]{4,3,2,1,0:T(8,128)}, f32[8,1,16]{2,1,0:T(1,128)S(1)}, f32[8,1,16,64,128]{4,3,2,1,0:T(8,128)}, /*index=5*/s32[]{:T(128)}, s32[]{:T(128)}) while((s32[]{:T(128)}, f32[1,16,64,128]{3,2,1,0:T(8,128)S(1)}, f32[8,1,16,64,128]{4,3,2,1,0:T(8,128)}, ...), condition=%wide.region_2.3_spmd.clone, body=%wide.region_1.2_spmd.clone.sunk | while | flops 524291 | bytes 2622240 | solution.py:93
  40.1 0.8 bitcast_dynamic-update-slice_fusion.2
  40.9 1.2 bitcast_add_fusion.2
  42.1 0.9 bitcast_dynamic-update-slice_fusion.2
  42.9 1.2 bitcast_add_fusion.2
  44.1 0.9 bitcast_dynamic-update-slice_fusion.2
  45.0 1.2 bitcast_add_fusion.2
  46.2 0.9 bitcast_dynamic-update-slice_fusion.2
  47.0 1.2 bitcast_add_fusion.2
  48.2 0.8 bitcast_dynamic-update-slice_fusion.2
  49.1 1.2 bitcast_add_fusion.2
  50.3 0.9 bitcast_dynamic-update-slice_fusion.2
  51.1 1.2 bitcast_add_fusion.2
  52.3 0.9 bitcast_dynamic-update-slice_fusion.2
  53.2 1.2 bitcast_add_fusion.2
  54.4 0.8 bitcast_dynamic-update-slice_fusion.2
  55.2 1.2 bitcast_add_fusion.2
  56.4 0.8 copy-done.3
  57.2 0.7 all-gather.8.cloned.1.call-update
  58.0 0.7 all-gather.10.cloned.1.call-update
  58.8 3.5 collective-permute-start.1
  62.3 0.7 dynamic-slice
  63.9 36.2 %all-reduce = f32[256]{0:T(256)S(1)} all-reduce(f32[256]{0:T(256)S(1)} %dynamic-update-slice), channel_id=2, replica_groups=mesh['ctx'=16,'head'=8] {'ctx'}, use_global_device_ids=true, to_apply=%add | all-reduce | flops 256 | bytes 2048
  100.3 0.6 gather_fusion
  100.9 0.6 gather_fusion.1
  102.3 4.0 %copy.91 = bf16[1024,1024]{0,1:T(8,128)(2,1)} copy(bf16[1024,1024]{1,0:T(8,128)(2,1)} %param.22) | data formatting | bytes 4194304 | tf_op args[3]
  107.0 1.6 copy-done.4
  108.6 3.1 copy.103
  111.7 3.5 fusion.21
  115.2 11.3 %fusion.4 = f32[8,16,64,128]{3,2,1,0:T(8,128)} fusion(f32[8,16,128]{2,1,0:T(8,128)S(1)} %copy.77, f32[8,16,128]{2,1,0:T(8,128)S(1)} %copy.75, f32[8,128,128]{2,1,0:T(8,128)S(1)} %fusion.61, pred[128,128]{1,0:T(8,128)(4,1)S(1)} %iota_compare_fusion, bf16[8,128,16,64]{1,0,3,2:T(8,128)(2,1)S(1)} %bitcast.172), kind=kOutput, calls=%fused_computation.11 | convolution fusion | flops 1621098496 | bytes 6963200 | tf_op jit(solution)/shard_map/cghqk,ckghp->cqghp/dot_general | solution.py:81
  126.5 2.2 all-gather.12.cloned.1.call-done
  128.7 12.8 %fusion.2 = f32[16,1,64,128]{3,1,2,0:T(1,128)S(1)} fusion(f32[16,16,1,1]{0,2,3,1:T(1,128)S(1)} %copy.95, f32[16,16,64,128]{3,2,1,0:T(8,128)} %all-gather.12.cloned.1.call-done), kind=kOutput, calls=%fused_computation.9 | convolution fusion | flops 25165824 | bytes 8913920 | tf_op jit(solution)/shard_map/jgh,jghpn->ghpn/dot_general | solution.py:109
  141.6 5.2 %fusion.19 = f32[8,128,1,16,64]{1,4,3,0,2:T(8,128)S(1)} fusion(f32[8,16,64,128]{3,2,1,0:T(8,128)S(1)} %copy-done.6, f32[8,16,64,128]{3,2,1,0:T(8,128)} %fusion.4, f32[8,128,1,16,64]{1,0,4,3,2:T(8,128)S(1)} %bitcast.169, f32[16,64,128,1]{2,1,0,3:T(8,128)S(1)} %bitcast.180, bf16[8,128,128,1]{2,1,3,0:T(8,128)(2,1)S(1)} %bitcast.176, f32[16]{0:T(128)S(1)} %copy-done.13, ...), kind=kOutput, calls=%fused_computation.35 | convolution fusion | flops 1616904192 | bytes 17694784 | tf_op jit(solution)/shard_map/cqgn,ghpn->cqghp/dot_general | solution.py:112
  146.8 3.3 copy.90
  150.1 4.0 %multiply_reduce_fusion.1 = (f32[1024]{0:T(1024)S(1)}, f32[1024,1024]{0,1:T(8,128)}) fusion(bf16[1024,1024]{0,1:T(8,128)(2,1)S(1)} %copy-done.7, f32[128,8,8,128]{3,2,1,0:T(8,128)S(1)} %bitcast.170), kind=kLoop, calls=%fused_computation.45 | loop fusion | flops 8387584 | bytes 10489856 | tf_op jit(solution)/shard_map/reduce_sum | solution.py:120
  154.2 66.4 %all-gather.8.cloned.1.call-done = bf16[96,1024,64]{1,2,0:T(8,128)(2,1)} async-done(((bf16[6,1024,64]{1,2,0:T(8,128)(2,1)}), bf16[96,1024,64]{1,2,0:T(8,128)(2,1)}) %all-gather.8.cloned.1.call-update) | async-done | bytes 12582928 | tf_op jit(solution)/shard_map/all_gather | solution.py:131
  220.5 5.1 %gather_fusion.2 = bf16[3,1024,64]{1,2,0:T(8,128)(2,1)S(1)} fusion(bf16[96,1024,64]{1,2,0:T(8,128)(2,1)} %all-gather.8.cloned.1.call-done, s32[1024]{0:T(1024)S(1)} %pad_clamp_fusion), kind=kCustom, calls=%fused_computation.2 | custom fusion | bytes 786444 | tf_op jit(solution)/shard_map/jit(_take)/gather | solution.py:134
  225.8 2.9 fusion.59
  228.7 0.8 multiply_reduce_fusion.2
  229.5 15.6 %convolution_convert_fusion = bf16[1024,4096]{1,0:T(8,128)(2,1)} fusion(bf16[1024,4096]{1,0:T(8,128)(2,1)} %param.30, f32[1024,1024]{0,1:T(8,128)} %get-tuple-element.84, f32[1024]{0:T(1024)S(1)} %convert_element_type.84, f32[1024]{0:T(1024)S(1)} %add_rsqrt_fusion), kind=kOutput, calls=%fused_computation.18 | convolution fusion | flops 8597274624 | bytes 20979712 | tf_op jit(solution)/shard_map/dot_general | solution.py:137
  245.1 38.6 %all-gather.10.cloned.1.call-done = bf16[96,64,512]{2,1,0:T(8,128)(2,1)} async-done(((bf16[6,64,512]{2,1,0:T(8,128)(2,1)}), bf16[96,64,512]{2,1,0:T(8,128)(2,1)}) %all-gather.10.cloned.1.call-update) | async-done | bytes 6291472 | tf_op jit(solution)/shard_map/all_gather | solution.py:132
  283.8 3.3 gather_fusion.3
  287.1 23.0 %all-gather.14.cloned.1.call-done = f32[8192,64]{0,1:T(8,128)} async-done(((f32[1024,64]{0,1:T(8,128)}), f32[8192,64]{0,1:T(8,128)}) %all-gather.14.cloned.1.call-update) | async-done | bytes 2097168 | tf_op jit(solution)/shard_map/all_gather | solution.py:148
  310.1 2.8 copy.105
  313.0 0.6 bitcast_reduce_fusion
  313.5 1.0 multiply_reduce_fusion
  314.6 50.5 %reduce-scatter.2.cloned.1.call-done = bf16[1024,512]{1,0:T(8,128)(2,1)} async-done(((bf16[1024,4096]{1,0:T(8,128)(2,1)}), bf16[1024,512]{1,0:T(8,128)(2,1)}) %reduce-scatter.2.cloned.1.call-update) | async-done | bytes 1048592 | tf_op jit(solution)/shard_map/reduce_scatter | solution.py:136
  365.1 2.6 add_convert_fusion
  (93 shorter events, 3.3 us)
Async XLA Ops:
  6.5 93.7 %copy-start = (s32[32]{0:T(128)S(1)}, s32[32]{0:T(128)}, u32[]{:S(2)}) copy-start(s32[32]{0:T(128)} %param.34) | copy-start | bytes 388
  6.5 21.5 %copy-start.9 = (bf16[1024,128]{1,0:T(8,128)(2,1)S(1)}, bf16[1024,128]{1,0:T(8,128)(2,1)}, u32[]{:S(2)}) copy-start(bf16[1024,128]{1,0:T(8,128)(2,1)} %param.20) | copy-start | bytes 786436
  6.5 122.1 %all-gather.12.cloned.1.call-start = ((), (), s32[]{:S(2)}) async-start(), calls=%async_computation.4 | async-start | bytes 8912896 | tf_op jit(solution)/shard_map/all_gather | solution.py:101
  8.2 20.3 %collective-permute-start = (bf16[3,1024]{0,1:T(8,128)(2,1)}, bf16[3,1024]{0,1:T(8,128)(2,1)S(1)}, u32[]{:S(2)}, u32[]{:S(2)}) collective-permute-start(bf16[3,1024]{0,1:T(8,128)(2,1)} %copy.73), channel_id=1, source_target_pairs={{0,8},{8,16},{16,24},{24,32},{32,40},{40,48},{48,56},{56,64},{64,7... | collective-permute-start | bytes 18440 | tf_op jit(solution)/shard_map/ppermute | solution.py:18
  12.8 15.2 %collective-permute-start.2 = (bf16[3,128]{1,0:T(4,128)(2,1)S(1)}, bf16[3,128]{1,0:T(4,128)(2,1)S(1)}, u32[]{:S(2)}, u32[]{:S(2)}) collective-permute-start(bf16[3,128]{1,0:T(4,128)(2,1)S(1)} %slice.104), channel_id=1, source_target_pairs={{0,8},{8,16},{16,24},{24,32},{32,40},{40,48},{48,56},{56,64},{64,7... | collective-permute-start | bytes 2312 | tf_op jit(solution)/shard_map/ppermute | solution.py:18
  40.0 18.7 %copy-start.10 = (bf16[1024,128]{1,0:T(8,128)(2,1)S(1)}, bf16[1024,128]{1,0:T(8,128)(2,1)}, u32[]{:S(2)}) copy-start(bf16[1024,128]{1,0:T(8,128)(2,1)} %param.21) | copy-start | bytes 786436
  40.0 22.3 %copy-start.15 = (u32[128]{0:T(128)S(1)}, u32[128]{0:T(128)}, u32[]{:S(2)}) copy-start(u32[128]{0:T(128)} %constant.114) | copy-start | bytes 1540
  40.0 60.9 %copy-start.2 = (s32[96]{0:T(128)S(1)}, s32[96]{0:T(128)}, u32[]{:S(2)}) copy-start(s32[96]{0:T(128)} %param.35) | copy-start | bytes 1156
  40.0 61.6 %copy-start.14 = (s32[32]{0:T(128)S(1)}, s32[32]{0:T(128)}, u32[]{:S(2)}) copy-start(s32[32]{0:T(128)} %param.33) | copy-start | bytes 388
  40.0 61.9 %copy-start.11 = (bf16[4,128]{1,0:T(4,128)(2,1)S(1)}, bf16[4,128]{1,0:T(4,128)(2,1)}, u32[]{:S(2)}) copy-start(bf16[4,128]{1,0:T(4,128)(2,1)} %param.28) | copy-start | bytes 3076
  56.4 0.8 copy-start.3
  56.4 49.9 %copy-start.12 = (bf16[1024]{0:T(1024)(128)(2,1)S(1)}, bf16[1024]{0:T(1024)(128)(2,1)}, u32[]{:S(2)}) copy-start(bf16[1024]{0:T(1024)(128)(2,1)} %param.29) | copy-start | bytes 6148
  57.2 163.3 %all-gather.8.cloned.1.call-start = ((), (), s32[]{:S(2)}) async-start(), calls=%async_computation.2 | async-start | bytes 13369344 | tf_op jit(solution)/shard_map/all_gather | solution.py:131
  57.9 225.8 %all-gather.10.cloned.1.call-start = ((), (), s32[]{:S(2)}) async-start(), calls=%async_computation.3 | async-start | bytes 6684672 | tf_op jit(solution)/shard_map/all_gather | solution.py:132
  58.7 251.4 %all-gather.14.cloned.1.call-start = ((), (), s32[]{:S(2)}) async-start(), calls=%async_computation.5 | async-start | bytes 2359296 | tf_op jit(solution)/shard_map/all_gather | solution.py:148
  58.8 47.5 %collective-permute-start.1 = (bf16[3,128]{1,0:T(4,128)(2,1)S(1)}, bf16[3,128]{1,0:T(4,128)(2,1)S(1)}, u32[]{:S(2)}, u32[]{:S(2)}) collective-permute-start(bf16[3,128]{1,0:T(4,128)(2,1)S(1)} %slice.95), channel_id=1, source_target_pairs={{0,8},{8,16},{16,24},{24,32},{32,40},{40,48},{48,56},{56,64},{64,7... | collective-permute-start | bytes 2312 | tf_op jit(solution)/shard_map/ppermute | solution.py:18
  106.3 2.4 copy-start.4
  108.6 3.1 copy-start.8
  126.5 15.1 %copy-start.13 = (f32[16]{0:T(128)S(1)}, f32[16]{0:T(128)}, u32[]{:S(2)}) copy-start(f32[16]{0:T(128)} %param.25) | copy-start | bytes 196
  128.7 12.9 %copy-start.5 = (f32[128,8,8,128]{3,2,1,0:T(8,128)S(1)}, f32[128,8,8,128]{3,2,1,0:T(8,128)}, u32[]{:S(2)}) copy-start(f32[128,8,8,128]{3,2,1,0:T(8,128)} %copy.103) | copy-start | bytes 12582916
  128.7 12.9 %copy-start.6 = (f32[8,16,64,128]{3,2,1,0:T(8,128)S(1)}, f32[8,16,64,128]{3,2,1,0:T(8,128)}, u32[]{:S(2)}) copy-start(f32[8,16,64,128]{3,2,1,0:T(8,128)} %fusion.21) | copy-start | bytes 12582916
  146.8 3.3 copy-start.7
  229.5 135.6 %reduce-scatter.2.cloned.1.call-start = ((), (), s32[]{:S(2)}) async-start(), calls=%async_computation.1 | async-start | bytes 9437184 | tf_op jit(solution)/shard_map/reduce_scatter | solution.py:136
  313.0 54.8 %copy-start.1 = (s32[32]{0:T(128)S(1)}, s32[32]{0:T(128)}, u32[]{:S(2)}) copy-start(s32[32]{0:T(128)} %param.34) | copy-start | bytes 388
Sparse Core Ops, SparseCore 0:
  57.3 71.3 all-gather.11
  130.9 89.6 all-gather.7
  222.7 60.9 all-gather.9
  285.3 24.7 all-gather.13
  312.3 52.7 reduce-scatter.1
